TPU v7x, 128 devices: a whole 4x4x4 slice. The times are simulated.
128 devices in a mesh: seq: 16 (over x, y_lo, core), tp: 8 (over z, y_hi).
Axes of the slice: x: 4, y: 4 (y_hi: 2, y_lo: 2; y = y_hi * 2 + y_lo), z: 4, core: 2. Of those that a mesh axis runs over, the one named last changes fastest.
Arguments:
- x_old: bfloat16 [8192, 4608], P('seq', 'tp'), may hold values from -6 to 6
- old_blocks: int32 [16], replicated, may hold values from 1 to 4, 32 in all
- new_blocks: int32 [16], replicated, may hold values from 1 to 4, 32 in all
- order: int32 [16], replicated, may hold values from 0 to 15, as said below
- pre_gain: float32 [4608], replicated, may hold values from 0.25 to 1.75
- post_gain: float32 [4608], replicated, may hold values from 0.25 to 1.75
- w_query: bfloat16 [4608, 4096], P('seq', 'tp'), may hold values from -0.59765625 to 0.59765625
- w_key: bfloat16 [4608, 2048], P('seq', 'tp'), may hold values from -0.09375 to 0.09375
- w_value: bfloat16 [4608, 2048], P('seq', 'tp'), may hold values from -0.09375 to 0.09375
- w_out_t: bfloat16 [4608, 4096], P('seq', 'tp'), may hold values from -0.09375 to 0.09375
Outputs:
- layer_out: bfloat16 [8192, 4608], P(('seq', 'tp'))
Inputs may be any that keep to these rules, and one draw needn't show every extreme that they name: `old_blocks`: counts of 128-row blocks, at least one each; they sum to 32, and the largest is exactly 4. `new_blocks`: counts of 128-row blocks, at least one each; they sum to 32, and the largest is exactly 4. A permutation of the seq indices with order[15] = 0 and order[7] = 15; the other indices, taken in increasing order, hold 1 to 14 in increasing order, except that aligned pairs of them (first and second, third and fourth, and so on) are swapped or not, pair by pair.
All inputs are finite; a program needn't handle non-finite values.
Results may differ from a plain program's by a relative error of at most 0.013.
Values may be sent and summed in bfloat16 or wider, within the bound.
A program may use at most 128 MiB of HBM per device.

v0:
```python
import math
import jax
import jax.numpy as jnp
from jax import lax
from jax.sharding import Mesh
from jax.sharding import PartitionSpec as P

D = 4608
HEADS = 32
HEAD = 128
BLOCK = 128
TP = ("tp_0", "tp_1")
SEQ_TP = ("seq", "tp_0", "tp_1")
EPS = 1e-06


def in_one_piece(arrays, axis, dim, along):
    widths = [a.shape[along] for a in arrays]
    both = jnp.concatenate(arrays, axis=along)
    whole = lax.all_gather(both, axis, axis=dim, tiled=True)
    return tuple(jnp.split(whole, [sum(widths[:k]) for k in range(1, len(widths))], axis=along))


def sum_by_axis(terms, axes):
    so_far = terms.astype(jnp.bfloat16)
    for axis in axes:
        so_far = lax.psum_scatter(so_far, axis, scatter_dimension=0, tiled=True)
    return so_far.astype(jnp.float32)


def offsets(blocks):
    return (jnp.cumsum(blocks) - blocks) * BLOCK


def rotate(values, places):
    half = values.shape[-1] // 2
    inverse = jnp.exp(
        jnp.arange(half, dtype=jnp.float32) * (-2.0 * math.log(10000.0) / values.shape[-1])
    )
    angles = places.astype(jnp.float32)[:, None] * inverse[None, :]
    cosine = jnp.cos(angles)[:, None, :]
    sine = jnp.sin(angles)[:, None, :]
    first = values[..., :half]
    second = values[..., half:]
    return jnp.concatenate(
        [first * cosine - second * sine, second * cosine + first * sine], axis=-1
    )


def rms_scale(values, gain):
    return values * lax.rsqrt(jnp.mean(values * values, axis=-1, keepdims=True) + EPS) * gain


def per_device(
    x_old, old_blocks, new_blocks, order, pre_gain, post_gain, w_query, w_key, w_value, w_out_t
):
    seq_count = lax.axis_size("seq")
    tp_count = lax.axis_size(TP)
    capacity = x_old.shape[0]
    seq_index = lax.axis_index("seq")
    tp_index = lax.axis_index(TP)
    old_start = offsets(old_blocks)
    new_start = offsets(new_blocks)
    new_count = new_blocks * BLOCK
    slot_ids = jnp.arange(capacity, dtype=jnp.int32)
    device_ids = jnp.arange(seq_count, dtype=jnp.int32)
    my_start = new_start[seq_index]
    my_count = new_count[seq_index]
    gathered = lax.all_gather(x_old, "seq", axis=0, tiled=True)
    wanted = my_start + slot_ids
    shard = jnp.sum((old_start[None, :] <= wanted[:, None]).astype(jnp.int32), axis=1) - 1
    match_shard = device_ids[None, :] == shard[:, None]
    holder = jnp.sum(
        device_ids[None, :] * (order[None, :] == shard[:, None]).astype(jnp.int32), axis=1
    )
    shard_start = jnp.sum(jnp.where(match_shard, old_start[None, :], 0), axis=1)
    source = jnp.clip(holder * capacity + wanted - shard_start, 0, seq_count * capacity - 1)
    own_rows = jnp.where(
        (slot_ids < my_count)[:, None], gathered[source], jnp.zeros((), jnp.bfloat16)
    )
    full_rows = lax.all_gather(own_rows, TP, axis=1, tiled=True)
    resident_f = full_rows.astype(jnp.float32)
    normed = rms_scale(resident_f, pre_gain).astype(jnp.bfloat16)
    query_full, key_full, value_full, out_full = in_one_piece(
        (w_query, w_key, w_value, w_out_t), "seq", 0, 1
    )
    query_raw = jnp.dot(normed, query_full, preferred_element_type=jnp.float32)
    key_raw = jnp.dot(normed, key_full, preferred_element_type=jnp.float32)
    value_raw = jnp.dot(normed, value_full, preferred_element_type=jnp.float32)
    local_heads = query_raw.shape[1] // HEAD
    local_kv = key_raw.shape[1] // HEAD
    group = local_heads // local_kv
    positions = my_start + slot_ids
    query_rot = (
        rotate(query_raw.reshape(capacity, local_heads, HEAD), positions) * (D // HEADS) ** (-0.5)
    ).astype(jnp.bfloat16)
    query_four = query_rot.reshape(capacity, local_kv, group, HEAD)
    key_rot = (
        rotate(key_raw.reshape(capacity, local_kv, HEAD), positions)
        .astype(jnp.bfloat16)
        .reshape(capacity, local_kv * HEAD)
    )
    value_b = value_raw.astype(jnp.bfloat16)
    start_state = (
        jnp.zeros((capacity, local_kv, group, HEAD), jnp.float32),
        jnp.zeros((local_kv, group, capacity), jnp.float32),
    )
    key_piece, value_piece = in_one_piece((key_rot, value_b), "seq", 0, 1)
    piece_rows = key_piece.shape[0]

    def one_block(carry_in, offset):
        numer, denom = carry_in
        key_block = lax.dynamic_slice_in_dim(key_piece, offset, capacity, 0).reshape(
            capacity, local_kv, HEAD
        )
        value_block = lax.dynamic_slice_in_dim(value_piece, offset, capacity, 0).reshape(
            capacity, local_kv, HEAD
        )
        global_ids = offset + jnp.arange(capacity, dtype=jnp.int32)
        owner = global_ids // capacity
        within = global_ids - owner * capacity
        onehot = owner[:, None] == device_ids[None, :]
        key_pos = jnp.sum(jnp.where(onehot, new_start[None, :], 0), axis=1) + within
        key_live = within < jnp.sum(jnp.where(onehot, new_count[None, :], 0), axis=1)
        allowed = key_live[None, :] & (key_pos[None, :] <= positions[:, None])
        score = jnp.einsum(
            "qcgd,kcd->cgqk", query_four, key_block, preferred_element_type=jnp.float32
        )
        weight = jnp.where(allowed[None, None, :, :], jnp.exp(50.0 * jnp.tanh(score / 50.0)), 0.0)
        denom = denom + jnp.sum(weight, axis=3)
        numer = numer + jnp.einsum(
            "cgqk,kcd->qcgd",
            weight.astype(jnp.bfloat16),
            value_block,
            preferred_element_type=jnp.float32,
        )
        return (numer, denom)

    numer, denom = lax.fori_loop(
        0,
        piece_rows // capacity,
        lambda turn, state: one_block(state, turn * capacity),
        start_state,
    )
    context = (
        (numer / jnp.transpose(denom, (2, 0, 1))[:, :, :, None])
        .astype(jnp.bfloat16)
        .reshape(capacity, local_heads * HEAD)
    )
    share = capacity // tp_count
    projected = sum_by_axis(
        lax.dot_general(
            context, out_full, (((1,), (1,)), ((), ())), preferred_element_type=jnp.float32
        ),
        TP,
    )
    first_row = tp_index * share
    residual = lax.dynamic_slice_in_dim(resident_f, first_row, share, 0)
    refreshed = residual + rms_scale(projected, post_gain)
    live = first_row + jnp.arange(share, dtype=jnp.int32) < my_count
    return jnp.where(live[:, None], refreshed, 0.0).astype(jnp.bfloat16)


def solution(mesh):
    torus = Mesh(mesh.devices.reshape(mesh.shape["seq"], 4, 2), ("seq", "tp_0", "tp_1"))
    in_specs = (
        P("seq", TP),
        P(),
        P(),
        P(),
        P(),
        P(),
        P("seq", TP),
        P("seq", TP),
        P("seq", TP),
        P("seq", TP),
    )
    out_specs = P(SEQ_TP, None)
    return jax.shard_map(
        per_device, mesh=torus, in_specs=in_specs, out_specs=out_specs, check_vma=False
    )
```

profile of v0, /device:TPU:1, one launch (start us, length us, event | category | flops | bytes accessed | tf_op | source)
XLA Modules:
  0.0 493.3 jit_solution(17339269859793845897)
XLA Ops:
  6.5 2.2 copy.36
  15.9 58.7 %all-gather.5.cloned.1.call-done = bf16[8192,576]{1,0:T(8,128)(2,1)} async-done(((bf16[512,576]{1,0:T(8,128)(2,1)}), bf16[8192,576]{1,0:T(8,128)(2,1)}) %all-gather.5.cloned.1.call-update) | async-done | bytes 9437200 | tf_op jit(solution)/shard_map/all_gather | solution.py:69
  74.6 7.5 %gather_fusion = bf16[512,576]{1,0:T(8,128)(2,1)S(1)} fusion(bf16[8192,576]{1,0:T(8,128)(2,1)} %all-gather.5.cloned.1.call-done, s32[1024]{0:T(1024)S(1)} %pad_clamp_fusion), kind=kCustom, calls=%fused_computation | custom fusion | bytes 1181696 | tf_op jit(solution)/shard_map/gather | solution.py:79
  85.0 73.8 %all-gather.7.cloned.1.call-done = bf16[512,4608]{0,1:T(8,128)(2,1)} async-done(((bf16[512,576]{0,1:T(8,128)(2,1)}), bf16[512,4608]{0,1:T(8,128)(2,1)}) %all-gather.7.cloned.1.call-update) | async-done | bytes 4718608 | tf_op jit(solution)/shard_map/all_gather | solution.py:81
  158.8 6.8 %copy.40 = bf16[512,4608]{1,0:T(8,128)(2,1)} copy(bf16[512,4608]{0,1:T(8,128)(2,1)} %all-gather.7.cloned.1.call-done) | data formatting | bytes 9437184 | tf_op jit(solution)/shard_map/all_gather | solution.py:81
  165.6 3.3 multiply_reduce_fusion
  168.9 69.7 %all-gather.9.cloned.1.call-done = bf16[4608,1536]{1,0:T(8,128)(2,1)} async-done(((bf16[288,1536]{1,0:T(8,128)(2,1)}), bf16[4608,1536]{1,0:T(8,128)(2,1)}) %all-gather.9.cloned.1.call-update) | async-done | bytes 14155792 | tf_op jit(solution)/shard_map/all_gather | solution.py:20
  238.6 4.8 fusion.32
  243.6 4.8 fusion.34
  249.5 6.5 %fusion.28 = f32[512,512]{0,1:T(8,128)S(1)} fusion(bf16[4608,1536]{1,0:T(8,128)(2,1)} %all-gather.9.cloned.1.call-done, f32[4608]{0:T(1024)S(1)} %copy-done.6, f32[512]{0:T(512)S(1)} %add_rsqrt_fusion, bf16[512,4608]{1,0:T(8,128)(2,1)} %copy.40), kind=kOutput, calls=%fused_computation.39 | convolution fusion | flops 2425356288 | bytes 10506240 | tf_op jit(solution)/shard_map/dot_general | solution.py:87
  257.3 45.0 %all-gather.11.cloned.1.call-done = bf16[8192,512]{0,1:T(8,128)(2,1)} async-done(((bf16[512,512]{0,1:T(8,128)(2,1)}), bf16[8192,512]{0,1:T(8,128)(2,1)}) %all-gather.11.cloned.1.call-update) | async-done | bytes 8388624 | tf_op jit(solution)/shard_map/all_gather | solution.py:20
  302.2 5.9 %fusion.44 = (bf16[8192,256]{0,1:T(8,128)(2,1)}, bf16[8192,256]{0,1:T(8,128)(2,1)}) fusion(bf16[8192,512]{0,1:T(8,128)(2,1)} %all-gather.11.cloned.1.call-done), kind=kLoop, calls=%fused_computation.84 | loop fusion | bytes 16777216 | tf_op jit(solution)/shard_map/split | solution.py:21
  308.2 88.0 %while.18 = (s32[]{:T(128)}, f32[512,2,2,128]{0,3,2,1:T(8,128)S(1)}, f32[2,2,512]{2,1,0:T(2,128)S(1)}, bf16[8192,256]{0,1:T(8,128)(2,1)}, s32[16]{0:T(128)S(1)},...) while((s32[]{:T(128)}, ...), condition=%wide.region_10.11_spmd.clone, body=%wide.region_6.10_spmd.clone.sunk | while | flops 546378240 | bytes 13423954 | solution.py:139
  309.1 1.1 constant_dynamic-slice_fusion.3
  310.2 1.8 fusion.63
  312.0 1.6 fusion.64
  314.6 1.1 constant_dynamic-slice_fusion.3
  315.7 1.8 fusion.63
  317.5 1.6 fusion.64
  320.1 1.1 constant_dynamic-slice_fusion.3
  321.2 1.8 fusion.63
  323.0 1.6 fusion.64
  325.6 1.1 constant_dynamic-slice_fusion.3
  326.7 1.8 fusion.63
  328.5 1.6 fusion.64
  331.1 1.1 constant_dynamic-slice_fusion.3
  332.2 1.8 fusion.63
  334.0 1.6 fusion.64
  336.6 1.1 constant_dynamic-slice_fusion.3
  337.7 1.8 fusion.63
  339.5 1.6 fusion.64
  342.1 1.1 constant_dynamic-slice_fusion.3
  343.2 1.8 fusion.63
  345.0 1.6 fusion.64
  347.6 1.1 constant_dynamic-slice_fusion.3
  348.7 1.8 fusion.63
  350.5 1.6 fusion.64
  353.1 1.1 constant_dynamic-slice_fusion.3
  354.2 1.8 fusion.63
  356.0 1.6 fusion.64
  358.6 1.1 constant_dynamic-slice_fusion.3
  359.7 1.8 fusion.63
  361.5 1.6 fusion.64
  364.1 1.1 constant_dynamic-slice_fusion.3
  365.2 1.8 fusion.63
  367.0 1.6 fusion.64
  369.6 1.1 constant_dynamic-slice_fusion.3
  370.7 1.8 fusion.63
  372.5 1.6 fusion.64
  376.2 1.8 fusion.63
  378.0 1.6 fusion.64
  380.6 1.1 constant_dynamic-slice_fusion.3
  381.7 1.8 fusion.63
  383.5 1.6 fusion.64
  387.2 1.8 fusion.63
  389.0 1.6 fusion.64
  392.7 1.8 fusion.63
  394.5 1.6 fusion.64
  396.3 6.7 %convolution_convert_fusion = bf16[512,4608]{1,0:T(8,128)(2,1)} fusion(bf16[512,512]{0,1:T(8,128)(2,1)S(1)} %bitcast.65, bf16[4608,1536]{1,0:T(8,128)(2,1)} %all-gather.9.cloned.1.call-done), kind=kOutput, calls=%fused_computation.37 | convolution fusion | flops 2418278400 | bytes 9961472 | tf_op jit(solution)/shard_map/dot_general | solution.py:152
  403.1 51.9 %reduce-scatter.3.cloned.1.call-done = bf16[128,4608]{1,0:T(8,128)(2,1)} async-done(((bf16[512,4608]{1,0:T(8,128)(2,1)}), bf16[128,4608]{1,0:T(8,128)(2,1)}) %reduce-scatter.3.cloned.1.call-update) | async-done | bytes 1179664 | tf_op jit(solution)/shard_map/reduce_scatter | solution.py:27
  455.6 7.2 %convert_element_type.53 = f32[512,4608]{1,0:T(8,128)} convert(bf16[512,4608]{1,0:T(8,128)(2,1)} %copy.40) | non-fusion elementwise | flops 2359296 | bytes 14155776 | tf_op jit(solution)/shard_map/convert_element_type | solution.py:82
  462.8 19.7 %reduce-scatter.5.cloned.1.call-done = bf16[64,4608]{1,0:T(8,128)(2,1)} async-done(((bf16[128,4608]{1,0:T(8,128)(2,1)}), bf16[64,4608]{1,0:T(8,128)(2,1)}) %reduce-scatter.5.cloned.1.call-update) | async-done | bytes 589840 | tf_op jit(solution)/shard_map/reduce_scatter | solution.py:27
  482.5 1.3 fusion.37
  483.9 2.6 fusion.41
  (161 shorter events, 31.7 us)
Async XLA Ops:
  6.5 68.0 %all-gather.5.cloned.1.call-start = ((), (), s32[]{:S(2)}) async-start(), calls=%async_computation.2 | async-start | bytes 11141120 | tf_op jit(solution)/shard_map/all_gather | solution.py:69
  8.7 74.6 %copy-start.1 = (bf16[288,512]{1,0:T(8,128)(2,1)S(1)}, bf16[288,512]{1,0:T(8,128)(2,1)}, u32[]{:S(2)}) copy-start(bf16[288,512]{1,0:T(8,128)(2,1)} %param.21) | copy-start | bytes 884740
  8.7 74.6 %copy-start.2 = (bf16[288,512]{1,0:T(8,128)(2,1)S(1)}, bf16[288,512]{1,0:T(8,128)(2,1)}, u32[]{:S(2)}) copy-start(bf16[288,512]{1,0:T(8,128)(2,1)} %param.18) | copy-start | bytes 884740
  8.8 74.6 %copy-start.3 = (bf16[288,256]{1,0:T(8,128)(2,1)S(1)}, bf16[288,256]{1,0:T(8,128)(2,1)}, u32[]{:S(2)}) copy-start(bf16[288,256]{1,0:T(8,128)(2,1)} %param.20) | copy-start | bytes 442372
  8.8 74.6 %copy-start.4 = (bf16[288,256]{1,0:T(8,128)(2,1)S(1)}, bf16[288,256]{1,0:T(8,128)(2,1)}, u32[]{:S(2)}) copy-start(bf16[288,256]{1,0:T(8,128)(2,1)} %param.19) | copy-start | bytes 442372
  8.8 150.0 %all-gather.7.cloned.1.call-start = ((), (), s32[]{:S(2)}) async-start(), calls=%async_computation.3 | async-start | bytes 5308416 | tf_op jit(solution)/shard_map/all_gather | solution.py:81
  83.3 155.3 %all-gather.9.cloned.1.call-start = ((), (), s32[]{:S(2)}) async-start(), calls=%async_computation.4 | async-start | bytes 15040512 | tf_op jit(solution)/shard_map/all_gather | solution.py:20
  84.4 217.9 %all-gather.11.cloned.1.call-start = ((), (), s32[]{:S(2)}) async-start(), calls=%async_computation.5 | async-start | bytes 8912896 | tf_op jit(solution)/shard_map/all_gather | solution.py:20
  165.6 73.0 %copy-start.6 = (f32[4608]{0:T(1024)S(1)}, f32[4608]{0:T(1024)}, u32[]{:S(2)}) copy-start(f32[4608]{0:T(1024)} %param.16) | copy-start | bytes 55300
  249.3 205.7 %reduce-scatter.3.cloned.1.call-start = ((), (), s32[]{:S(2)}) async-start(), calls=%async_computation.6 | async-start | bytes 5898240 | tf_op jit(solution)/shard_map/reduce_scatter | solution.py:27
  257.3 50.9 %copy-start = (f32[512,2,2,128]{0,3,2,1:T(8,128)S(1)}, f32[512,2,2,128]{0,3,2,1:T(8,128)}, u32[]{:S(2)}) copy-start(f32[512,2,2,128]{0,3,2,1:T(8,128)} %custom-call) | copy-start | bytes 3145732
  403.0 79.5 %reduce-scatter.5.cloned.1.call-start = ((), (), s32[]{:S(2)}) async-start(), calls=%async_computation.7 | async-start | bytes 1769472 | tf_op jit(solution)/shard_map/reduce_scatter | solution.py:27
  455.6 28.2 %copy-start.5 = (f32[4608]{0:T(1024)S(1)}, f32[4608]{0:T(1024)}, u32[]{:S(2)}) copy-start(f32[4608]{0:T(1024)} %param.17) | copy-start | bytes 55300
Sparse Core Ops, SparseCore 0:
  9.0 65.4 all-gather.4
  83.4 75.3 all-gather.6
  160.5 78.0 all-gather.8
  249.4 52.8 all-gather.10
  403.1 51.7 reduce-scatter.2
  457.1 25.3 reduce-scatter.4
where the time goes:
time: 494 us; the launch traced here: 493 us
  waiting for transfers between devices  319 us (65%)
  matrix products  77.3 us (16%)
  local copies, waits for them, and re-layouts  44 us (9%)
  other arithmetic  37.9 us (8%)
  between operations  13.8 us (3%)
    all_gather x2, waiting for transfers between devices, in_one_piece(): whole = lax.all_gather(both, axis, axis=dim, tiled=True)  115 us
    all_gather x1, waiting for transfers between devices, per_device(): full_rows = lax.all_gather(own_rows, TP, axis=1, tiled=True)  73.8 us
    reduce_scatter x2, waiting for transfers between devices, sum_by_axis(): so_far = lax.psum_scatter(so_far, axis, scatter_dimension=0, tiled=True)  71.6 us
    all_gather x1, waiting for transfers between devices, per_device(): gathered = lax.all_gather(x_old, 'seq', axis=0, tiled=True)  58.7 us
    dot_general x16, matrix products, one_block(): jnp.einsum('qcgd,kcd->cgqk', query_four, key_block, preferred_element_typ...  28.1 us
    dot_general x16, matrix products, one_block(): jnp.einsum('cgqk,kcd->qcgd', weight.astype(jnp.bfloat16), value_block, pr...  26.3 us
    dynamic_slice x16, local copies, waits for them, and re-layouts, one_block(): lax.dynamic_slice_in_dim(key_piece, offset, capacity, 0)  17.2 us
    add x17, other arithmetic, per_device(): wanted = my_start + slot_ids  9.9 us
  transfers between devices with their start and end apart: 6, of which 6 were waited for; matrix products, arithmetic and copies ran while one was open for 7% of the time, Pallas kernels for 0%

commit v1 on v0

--- a/solution.py
+++ b/solution.py
@@ -12,6 +12,13 @@
 TP = ("tp_0", "tp_1")
 SEQ_TP = ("seq", "tp_0", "tp_1")
 EPS = 1e-06
+
+
+def all_by_exchange(array, mesh_axis, along):
+    size = lax.axis_size(mesh_axis)
+    blocks = jnp.stack([array for _ in range(size)])
+    blocks = lax.all_to_all(blocks, mesh_axis, split_axis=0, concat_axis=0)
+    return jnp.concatenate(blocks, axis=along)
 
 
 def in_one_piece(arrays, axis, dim, along):
@@ -66,7 +73,7 @@
     device_ids = jnp.arange(seq_count, dtype=jnp.int32)
     my_start = new_start[seq_index]
     my_count = new_count[seq_index]
-    gathered = lax.all_gather(x_old, "seq", axis=0, tiled=True)
+    gathered = all_by_exchange(x_old, "seq", 0)
     wanted = my_start + slot_ids
     shard = jnp.sum((old_start[None, :] <= wanted[:, None]).astype(jnp.int32), axis=1) - 1
     match_shard = device_ids[None, :] == shard[:, None]

time: 494 us -> 663 us (1.34)
  waiting for transfers between devices: 319 us -> 407 us
  matrix products: 77.3 us -> 137 us
  local copies, waits for them, and re-layouts: 44 us -> 60.2 us
  starting transfers between devices: 0.39 us -> 7.33 us
    all_to_all x0 -> x1, waiting for transfers between devices: none -> 145 us  [all_by_exchange(): blocks = lax.all_to_all(blocks, mesh_axis, split_axis=0, concat_axis=0)]
    all_gather x1 -> x0, waiting for transfers between devices: 58.7 us -> none  [per_device(): gathered = lax.all_gather(x_old, 'seq', axis=0, tiled=True)]
    dot_general x16, matrix products: 26.3 us -> 59.2 us  [one_block(): jnp.einsum('cgqk,kcd->qcgd', weight.astype(jnp.bfloat16), value_block, pr...]
    dot_general x16, matrix products: 28.1 us -> 54.5 us  [one_block(): jnp.einsum('qcgd,kcd->cgqk', query_four, key_block, preferred_element_typ...]
    all_to_all x0 -> x1, local copies, waits for them, and re-layouts: none -> 14.1 us  [all_by_exchange(): blocks = lax.all_to_all(blocks, mesh_axis, split_axis=0, concat_axis=0)]
    all_to_all x0 -> x1, starting transfers between devices: none -> 6.95 us  [all_by_exchange(): blocks = lax.all_to_all(blocks, mesh_axis, split_axis=0, concat_axis=0)]
  transfers between devices with their start and end apart: 6 -> 6, of which waited for: 6 -> 6; matrix products, arithmetic and copies ran while one was open for 7% -> 5% of each run, Pallas kernels for 0% -> 0%
where the time goes in v1:
time: 663 us; the launch traced here: 662 us
  waiting for transfers between devices  407 us (61%)
  matrix products  137 us (21%)
  local copies, waits for them, and re-layouts  60.2 us (9%)
  other arithmetic  36 us (5%)
  between operations  13.4 us (2%)
  starting transfers between devices  7.33 us (1%)
    all_to_all x1, waiting for transfers between devices, all_by_exchange(): blocks = lax.all_to_all(blocks, mesh_axis, split_axis=0, concat_axis=0)  145 us
    all_gather x2, waiting for transfers between devices, in_one_piece(): whole = lax.all_gather(both, axis, axis=dim, tiled=True)  115 us
    all_gather x1, waiting for transfers between devices, per_device(): full_rows = lax.all_gather(own_rows, TP, axis=1, tiled=True)  76.3 us
    reduce_scatter x2, waiting for transfers between devices, sum_by_axis(): so_far = lax.psum_scatter(so_far, axis, scatter_dimension=0, tiled=True)  71.6 us
    dot_general x16, matrix products, one_block(): jnp.einsum('cgqk,kcd->qcgd', weight.astype(jnp.bfloat16), value_block, pr...  59.2 us
    dot_general x16, matrix products, one_block(): jnp.einsum('qcgd,kcd->cgqk', query_four, key_block, preferred_element_typ...  54.5 us
    dynamic_slice x16, local copies, waits for them, and re-layouts, one_block(): lax.dynamic_slice_in_dim(key_piece, offset, capacity, 0)  17.1 us
    all_to_all x1, local copies, waits for them, and re-layouts, all_by_exchange(): blocks = lax.all_to_all(blocks, mesh_axis, split_axis=0, concat_axis=0)  14.1 us
  transfers between devices with their start and end apart: 6, of which 6 were waited for; matrix products, arithmetic and copies ran while one was open for 5% of the time, Pallas kernels for 0%

profile of v1, /device:TPU:1, one launch (start us, length us, event | category | flops | bytes accessed | tf_op | source)
XLA Modules:
  0.0 661.5 jit_solution(13024424873327461294)
XLA Ops:
  6.5 5.6 stack.2
  12.1 6.9 %all-to-all-start = ((bf16[16,512,576]{1,2,0:T(8,128)(2,1)}), bf16[16,512,576]{1,2,0:T(8,128)(2,1)}, u32[]{:S(2)}, u32[]{:S(2)}) async-start(bf16[16,512,576]{1,2,0:T(8,128)(2,1)} %stack.2), calls=%async_computation | async-start | bytes 18874368 | tf_op jit(solution)/shard_map/all_to_all | solution.py:20
  22.9 144.5 %all-to-all-done = bf16[16,512,576]{1,2,0:T(8,128)(2,1)} async-done(((bf16[16,512,576]{1,2,0:T(8,128)(2,1)}), bf16[16,512,576]{1,2,0:T(8,128)(2,1)}, u32[]{:S(2)}, u32[]{:S(2)}) %all-to-all-start) | async-done | bytes 9437216 | tf_op jit(solution)/shard_map/all_to_all | solution.py:20
  167.4 14.1 %copy.36 = bf16[16,512,576]{2,1,0:T(8,128)(2,1)} copy(bf16[16,512,576]{1,2,0:T(8,128)(2,1)} %all-to-all-done) | data formatting | bytes 18874368 | tf_op jit(solution)/shard_map/all_to_all | solution.py:20
  181.5 7.5 %gather_fusion = bf16[512,576]{1,0:T(8,128)(2,1)S(1)} fusion(bf16[8192,576]{1,0:T(8,128)(2,1)} %bitcast.60, s32[1024]{0:T(1024)S(1)} %pad_clamp_fusion), kind=kCustom, calls=%fused_computation | custom fusion | bytes 1181696 | tf_op jit(solution)/shard_map/gather | solution.py:86
  192.0 76.3 %all-gather.4.cloned.1.call-done = bf16[512,4608]{0,1:T(8,128)(2,1)} async-done(((bf16[512,576]{0,1:T(8,128)(2,1)}), bf16[512,4608]{0,1:T(8,128)(2,1)}) %all-gather.4.cloned.1.call-update) | async-done | bytes 4718608 | tf_op jit(solution)/shard_map/all_gather | solution.py:88
  268.3 6.8 %copy.40 = bf16[512,4608]{1,0:T(8,128)(2,1)} copy(bf16[512,4608]{0,1:T(8,128)(2,1)} %all-gather.4.cloned.1.call-done) | data formatting | bytes 9437184 | tf_op jit(solution)/shard_map/all_gather | solution.py:88
  275.0 3.3 multiply_reduce_fusion
  278.4 69.7 %all-gather.6.cloned.1.call-done = bf16[4608,1536]{1,0:T(8,128)(2,1)} async-done(((bf16[288,1536]{1,0:T(8,128)(2,1)}), bf16[4608,1536]{1,0:T(8,128)(2,1)}) %all-gather.6.cloned.1.call-update) | async-done | bytes 14155792 | tf_op jit(solution)/shard_map/all_gather | solution.py:27
  348.1 4.8 fusion.32
  353.0 4.8 fusion.34
  359.0 6.5 fusion.28
  366.7 45.0 %all-gather.8.cloned.1.call-done = bf16[8192,512]{0,1:T(8,128)(2,1)} async-done(((bf16[512,512]{0,1:T(8,128)(2,1)}), bf16[8192,512]{0,1:T(8,128)(2,1)}) %all-gather.8.cloned.1.call-update) | async-done | bytes 8388624 | tf_op jit(solution)/shard_map/all_gather | solution.py:27
  411.7 5.9 fusion.44
  417.7 147.1 %while.18 = (s32[]{:T(128)}, f32[512,2,2,128]{0,3,2,1:T(8,128)S(1)}, f32[2,2,512]{2,1,0:T(2,128)S(1)}, bf16[8192,256]{0,1:T(8,128)(2,1)}, s32[16]{0:T(128)S(1)},...) while((s32[]{:T(128)}, ...), condition=%wide.region_10.11_spmd.clone, body=%wide.region_6.10_spmd.clone.sunk | while | flops 546378240 | bytes 13423946 | solution.py:146
  418.6 1.1 constant_dynamic-slice_fusion.3
  419.7 3.4 fusion.63
  423.1 3.7 fusion.64
  428.9 3.4 fusion.63
  432.3 3.7 fusion.64
  437.0 1.1 constant_dynamic-slice_fusion.3
  438.1 3.4 fusion.63
  441.5 3.7 fusion.64
  446.2 1.1 constant_dynamic-slice_fusion.3
  447.3 3.4 fusion.63
  450.7 3.7 fusion.64
  455.4 1.1 constant_dynamic-slice_fusion.3
  456.5 3.4 fusion.63
  459.9 3.7 fusion.64
  464.6 1.1 constant_dynamic-slice_fusion.3
  465.7 3.4 fusion.63
  469.1 3.7 fusion.64
  473.8 1.1 constant_dynamic-slice_fusion.3
  474.9 3.4 fusion.63
  478.3 3.7 fusion.64
  483.0 1.1 constant_dynamic-slice_fusion.3
  484.1 3.4 fusion.63
  487.5 3.7 fusion.64
  492.2 1.1 constant_dynamic-slice_fusion.3
  493.3 3.4 fusion.63
  496.7 3.7 fusion.64
  501.4 1.1 constant_dynamic-slice_fusion.3
  502.4 3.4 fusion.63
  505.9 3.7 fusion.64
  510.6 1.1 constant_dynamic-slice_fusion.3
  511.6 3.4 fusion.63
  515.1 3.7 fusion.64
  519.8 1.1 constant_dynamic-slice_fusion.3
  520.8 3.4 fusion.63
  524.2 3.7 fusion.64
  530.0 3.4 fusion.63
  533.4 3.7 fusion.64
  539.2 3.4 fusion.63
  542.6 3.7 fusion.64
  548.4 3.4 fusion.63
  551.8 3.7 fusion.64
  557.6 3.4 fusion.63
  561.0 3.7 fusion.64
  564.9 6.7 %convolution_convert_fusion = bf16[512,4608]{1,0:T(8,128)(2,1)} fusion(bf16[512,512]{0,1:T(8,128)(2,1)S(1)} %bitcast.67, bf16[4608,1536]{1,0:T(8,128)(2,1)} %all-gather.6.cloned.1.call-done), kind=kOutput, calls=%fused_computation.37 | convolution fusion | flops 2418278400 | bytes 9961472 | tf_op jit(solution)/shard_map/dot_general | solution.py:159
  571.7 51.9 %reduce-scatter.3.cloned.1.call-done = bf16[128,4608]{1,0:T(8,128)(2,1)} async-done(((bf16[512,4608]{1,0:T(8,128)(2,1)}), bf16[128,4608]{1,0:T(8,128)(2,1)}) %reduce-scatter.3.cloned.1.call-update) | async-done | bytes 1179664 | tf_op jit(solution)/shard_map/reduce_scatter | solution.py:34
  624.2 7.2 %convert_element_type.53 = f32[512,4608]{1,0:T(8,128)} convert(bf16[512,4608]{1,0:T(8,128)(2,1)} %copy.40) | non-fusion elementwise | flops 2359296 | bytes 14155776 | tf_op jit(solution)/shard_map/convert_element_type | solution.py:89
  631.4 19.7 %reduce-scatter.5.cloned.1.call-done = bf16[64,4608]{1,0:T(8,128)(2,1)} async-done(((bf16[128,4608]{1,0:T(8,128)(2,1)}), bf16[64,4608]{1,0:T(8,128)(2,1)}) %reduce-scatter.5.cloned.1.call-update) | async-done | bytes 589840 | tf_op jit(solution)/shard_map/reduce_scatter | solution.py:34
  651.1 1.3 fusion.37
  652.4 2.6 fusion.41
  (167 shorter events, 30.5 us)
Async XLA Ops:
  12.1 7.0 %copy-start.6 = (s32[16]{0:T(128)S(1)}, s32[16]{0:T(128)}, u32[]{:S(2)}) copy-start(s32[16]{0:T(128)} %param.14) | copy-start | bytes 196
  12.1 7.3 %copy-start.8 = (s32[16]{0:T(128)S(1)}, s32[16]{0:T(128)}, u32[]{:S(2)}) copy-start(s32[16]{0:T(128)} %param.13) | copy-start | bytes 196
  12.1 10.0 %copy-start.7 = (s32[16]{0:T(128)S(1)}, s32[16]{0:T(128)}, u32[]{:S(2)}) copy-start(s32[16]{0:T(128)} %param.15) | copy-start | bytes 196
  12.1 155.3 %all-to-all-start = ((bf16[16,512,576]{1,2,0:T(8,128)(2,1)}), bf16[16,512,576]{1,2,0:T(8,128)(2,1)}, u32[]{:S(2)}, u32[]{:S(2)}) async-start(bf16[16,512,576]{1,2,0:T(8,128)(2,1)} %stack.2), calls=%async_computation | async-start | bytes 18874368 | tf_op jit(solution)/shard_map/all_to_all | solution.py:20
  19.1 249.2 %all-gather.4.cloned.1.call-start = ((), (), s32[]{:S(2)}) async-start(), calls=%async_computation.3 | async-start | bytes 5308416 | tf_op jit(solution)/shard_map/all_gather | solution.py:88
  181.5 8.9 %copy-start.1 = (bf16[288,512]{1,0:T(8,128)(2,1)S(1)}, bf16[288,512]{1,0:T(8,128)(2,1)}, u32[]{:S(2)}) copy-start(bf16[288,512]{1,0:T(8,128)(2,1)} %param.21) | copy-start | bytes 884740
  181.5 8.9 %copy-start.2 = (bf16[288,512]{1,0:T(8,128)(2,1)S(1)}, bf16[288,512]{1,0:T(8,128)(2,1)}, u32[]{:S(2)}) copy-start(bf16[288,512]{1,0:T(8,128)(2,1)} %param.18) | copy-start | bytes 884740
  181.5 8.9 %copy-start.3 = (bf16[288,256]{1,0:T(8,128)(2,1)S(1)}, bf16[288,256]{1,0:T(8,128)(2,1)}, u32[]{:S(2)}) copy-start(bf16[288,256]{1,0:T(8,128)(2,1)} %param.20) | copy-start | bytes 442372
  181.5 8.9 %copy-start.4 = (bf16[288,256]{1,0:T(8,128)(2,1)S(1)}, bf16[288,256]{1,0:T(8,128)(2,1)}, u32[]{:S(2)}) copy-start(bf16[288,256]{1,0:T(8,128)(2,1)} %param.19) | copy-start | bytes 442372
  190.3 157.7 %all-gather.6.cloned.1.call-start = ((), (), s32[]{:S(2)}) async-start(), calls=%async_computation.4 | async-start | bytes 15040512 | tf_op jit(solution)/shard_map/all_gather | solution.py:27
  191.4 220.3 %all-gather.8.cloned.1.call-start = ((), (), s32[]{:S(2)}) async-start(), calls=%async_computation.5 | async-start | bytes 8912896 | tf_op jit(solution)/shard_map/all_gather | solution.py:27
  275.0 73.0 %copy-start.9 = (f32[4608]{0:T(1024)S(1)}, f32[4608]{0:T(1024)}, u32[]{:S(2)}) copy-start(f32[4608]{0:T(1024)} %param.16) | copy-start | bytes 55300
  358.7 264.8 %reduce-scatter.3.cloned.1.call-start = ((), (), s32[]{:S(2)}) async-start(), calls=%async_computation.6 | async-start | bytes 5898240 | tf_op jit(solution)/shard_map/reduce_scatter | solution.py:34
  366.7 51.0 %copy-start = (f32[512,2,2,128]{0,3,2,1:T(8,128)S(1)}, f32[512,2,2,128]{0,3,2,1:T(8,128)}, u32[]{:S(2)}) copy-start(f32[512,2,2,128]{0,3,2,1:T(8,128)} %custom-call) | copy-start | bytes 3145732
  571.6 79.5 %reduce-scatter.5.cloned.1.call-start = ((), (), s32[]{:S(2)}) async-start(), calls=%async_computation.7 | async-start | bytes 1769472 | tf_op jit(solution)/shard_map/reduce_scatter | solution.py:34
  624.2 28.2 %copy-start.5 = (f32[4608]{0:T(1024)S(1)}, f32[4608]{0:T(1024)}, u32[]{:S(2)}) copy-start(f32[4608]{0:T(1024)} %param.17) | copy-start | bytes 55300
Sparse Core Ops, SparseCore 0:
  190.5 77.7 all-gather.3
  270.0 78.0 all-gather.5
  358.8 52.8 all-gather.7
  571.8 51.7 reduce-scatter.2
  625.8 25.3 reduce-scatter.4
